TPU v7x, 32 devices: a whole 2x2x4 slice. The times are simulated.
32 devices in a mesh: pb: 4 (over y, core), pa: 8 (over z, x).
Axes of the slice: x: 2, y: 2, z: 4, core: 2. Of those that a mesh axis runs over, the one named last changes fastest.
Arguments:
- query_hidden: bfloat16 [32, 32, 2048], P('pb', 'pa'), may hold values from -32 to 32
- page_hidden: bfloat16 [8, 1024, 2048], P('pa', 'pb'), may hold values from -4.2 to 4.2
- projection: bfloat16 [2048, 128], replicated, may hold values from -0.125 to 0.125
- clicks: int32 [32, 8, 2], P('pb'), may hold values from 0 to 7, as said below
- bins: int32 [32, 8], P('pb'), may hold values from 0 to 7
Outputs:
- query_grad: bfloat16 [32, 32, 2048], P('pb', 'pa')
- page_grad: bfloat16 [8, 1024, 2048], P('pa', 'pb')
- weight_grad: float32 [2048, 128], P(('pb', 'pa'))
Inputs may be any that keep to these rules, and one draw needn't show every extreme that they name: `clicks`: the two pages of a pair always differ.
All inputs are finite; a program needn't handle non-finite values.
Results may differ from a plain program's by a relative error of at most 0.019.
Values may be sent and summed in bfloat16 or wider, within the bound.
A program may use at most 64 MiB of HBM per device.

v0:
```python
import jax
import jax.numpy as jnp
from jax import lax
from jax.sharding import PartitionSpec as P

sharpness = 0.25


def from_behind(value, axis, steps):
    count = lax.axis_size(axis)
    pairs = [(source, (source + steps) % count) for source in range(count)]
    return lax.ppermute(value, axis, pairs)


def logits(token_rows, patch_rows):
    return sharpness * lax.dot_general(
        token_rows, patch_rows, (((1,), (1,)), ((), ())), preferred_element_type=jnp.float32
    )


def shards(query_hidden, page_hidden, projection, clicks, bins):
    query_count, token_local, hidden_width = query_hidden.shape
    page_count, patch_local, _ = page_hidden.shape
    embed_width = projection.shape[1]
    own_embed = jnp.dot(
        query_hidden.reshape(-1, hidden_width), projection, preferred_element_type=jnp.float32
    ).astype(jnp.bfloat16)
    own_embed = own_embed.reshape(query_count, token_local, embed_width)
    tok_rows = lax.all_gather(own_embed, "pa", axis=1, tiled=True).reshape(-1, embed_width)
    row_count = tok_rows.shape[0]
    query_tokens = row_count // query_count
    page_embed = jnp.dot(
        page_hidden.reshape(-1, hidden_width), projection, preferred_element_type=jnp.float32
    ).astype(jnp.bfloat16)
    page_embed = page_embed.reshape(page_count, patch_local, embed_width)
    start_state = (
        jnp.full((row_count, page_count), -1e30, jnp.float32),
        jnp.zeros((row_count, page_count), jnp.float32),
    )
    run_max, run_sum = start_state
    logit_block = logits(tok_rows, lax.all_gather(page_embed, "pb", axis=1, tiled=True)[0])
    new_max = jnp.maximum(run_max[:, 0], jnp.max(logit_block, axis=1))
    new_sum = run_sum[:, 0] * jnp.exp(run_max[:, 0] - new_max)
    new_sum = new_sum + jnp.sum(jnp.exp(logit_block - new_max[:, None]), axis=1)
    max_list = [new_max]
    sum_list = [new_sum]
    run_max = jnp.stack(max_list, axis=1)
    run_sum = jnp.stack(sum_list, axis=1)
    log_norm = run_max + jnp.log(run_sum)
    query_score = log_norm.reshape(query_count, query_tokens, page_count).sum(axis=1)
    owned_pages = lax.axis_index("pa") * page_count + jnp.arange(page_count, dtype=jnp.int32)
    positive = clicks[:, :, 0]
    negative = clicks[:, :, 1]
    hit_pos = (positive[:, :, None] == owned_pages).astype(jnp.float32)
    hit_neg = (negative[:, :, None] == owned_pages).astype(jnp.float32)
    score_table = lax.all_gather(query_score, "pa", axis=1, tiled=True)
    page_ids = jnp.arange(score_table.shape[1], dtype=jnp.int32)
    table_pos = (positive[:, :, None] == page_ids).astype(jnp.float32)
    table_neg = (negative[:, :, None] == page_ids).astype(jnp.float32)
    pair_gap = jnp.sum(table_pos * score_table[:, None, :], axis=2) - jnp.sum(
        table_neg * score_table[:, None, :], axis=2
    )
    pair_weight = jnp.sqrt(bins.astype(jnp.float32) + 1.0)
    pair_coeff = -pair_weight * jax.nn.sigmoid(-pair_gap)
    score_grad = jnp.sum(pair_coeff[:, :, None] * (hit_pos - hit_neg), axis=1)
    grad_rows = jnp.repeat(score_grad, query_tokens, axis=0)
    norm_cols = jnp.repeat(log_norm, patch_local, axis=1)
    grad_cols = jnp.repeat(grad_rows, patch_local, axis=1)

    def cycle_turn(turn_index, cycle_state):
        patch_block, patch_accum, token_acc = cycle_state
        block_rows = patch_block.reshape(-1, embed_width)
        logit_block = logits(tok_rows, block_rows)
        soft_grad = (grad_cols * jnp.exp(logit_block - norm_cols)).astype(jnp.bfloat16)
        token_acc = token_acc + jnp.dot(soft_grad, block_rows, preferred_element_type=jnp.float32)
        patch_part = lax.dot_general(
            soft_grad, tok_rows, (((0,), (0,)), ((), ())), preferred_element_type=jnp.float32
        )
        patch_accum = patch_accum + patch_part.reshape(patch_accum.shape)
        patch_block = from_behind(patch_block, "pb", 1)
        patch_accum = from_behind(patch_accum.astype(jnp.bfloat16), "pb", 1).astype(
            patch_accum.dtype
        )
        return (patch_block, patch_accum, token_acc)

    start_state = (
        page_embed,
        jnp.zeros(page_embed.shape, jnp.float32),
        jnp.zeros((row_count, embed_width), jnp.float32),
    )
    _, patch_acc, token_acc = lax.fori_loop(0, lax.axis_size("pb"), cycle_turn, start_state)
    token_own = lax.psum_scatter(
        token_acc.reshape(query_count, query_tokens, embed_width).astype(jnp.bfloat16),
        "pa",
        scatter_dimension=1,
        tiled=True,
    ).astype(jnp.float32)
    token_low = (sharpness * token_own).astype(jnp.bfloat16).reshape(-1, embed_width)
    patch_low = (sharpness * patch_acc).astype(jnp.bfloat16).reshape(-1, embed_width)
    query_grad = lax.dot_general(
        token_low, projection, (((1,), (1,)), ((), ())), preferred_element_type=jnp.float32
    )
    query_grad = query_grad.astype(jnp.bfloat16).reshape(query_hidden.shape)
    page_grad = lax.dot_general(
        patch_low, projection, (((1,), (1,)), ((), ())), preferred_element_type=jnp.float32
    )
    page_grad = page_grad.astype(jnp.bfloat16).reshape(page_hidden.shape)
    weight_term = lax.dot_general(
        query_hidden.reshape(-1, hidden_width),
        token_low,
        (((0,), (0,)), ((), ())),
        preferred_element_type=jnp.float32,
    )
    weight_term = weight_term + lax.dot_general(
        page_hidden.reshape(-1, hidden_width),
        patch_low,
        (((0,), (0,)), ((), ())),
        preferred_element_type=jnp.float32,
    )
    weight_grad = lax.psum_scatter(weight_term, ("pb", "pa"), scatter_dimension=0, tiled=True)
    return (query_grad, page_grad, weight_grad)


def solution(mesh):
    return jax.shard_map(
        shards,
        mesh=mesh,
        in_specs=(
            P("pb", "pa", None),
            P("pa", "pb", None),
            P(),
            P("pb", None, None),
            P("pb", None),
        ),
        out_specs=(P("pb", "pa", None), P("pa", "pb", None), P(("pb", "pa"), None)),
        check_vma=False,
    )
```

profile of v0, /device:TPU:0, one launch (start us, length us, event | category | flops | bytes accessed | tf_op | source)
XLA Modules:
  0.0 294.6 jit_solution(1814558097921956855)
XLA Ops:
  7.2 1.2 copy-done
  8.4 1.5 convolution_convert_fusion.2
  9.9 7.3 %all-gather = bf16[1024,128]{1,0:T(8,128)(2,1)S(1)} all-gather(bf16[256,128]{1,0:T(8,128)(2,1)S(1)} %convolution_convert_fusion.2), channel_id=2, replica_groups=mesh['pb'=4,'pa'=8] {'pb'}, dimensions={0}, use_global_device_ids=true | all-gather | bytes 327680 | tf_op jit(solution)/shard_map/all_gather | solution.py:41
  17.5 30.9 %all_gather.9 = bf16[8,32,128]{2,0,1:T(8,128)(2,1)S(1)} all-gather(bf16[8,4,128]{2,0,1:T(8,128)(2,1)S(1)} %copy.36), channel_id=1, replica_groups=mesh['pb'=4,'pa'=8] {'pa'}, dimensions={1}, use_global_device_ids=true | all-gather | bytes 73728 | tf_op jit(solution)/shard_map/all_gather | solution.py:29
  48.4 0.4 fusion.24
  48.8 0.3 exponential_reduce_fusion
  49.4 20.5 %all-gather.1 = f32[8,1,8]{2,1,0:T(1,128)S(1)} all-gather(f32[1,1,8]{2,1,0:T(1,128)S(1)} %bitcast.83), channel_id=1, replica_groups=mesh['pb'=4,'pa'=8] {'pa'}, dimensions={0}, use_global_device_ids=true | all-gather | bytes 288 | tf_op jit(solution)/shard_map/all_gather | solution.py:56
  70.4 18.0 %while.15 = (s32[]{:T(128)}, bf16[1,256,128]{2,1,0:T(8,128)(2,1)S(1)}, f32[1,256,128]{2,1,0:T(8,128)S(1)}, f32[256,128]{1,0:T(8,128)S(1)}, bf16[256,128]{1,0:T(8...) while((s32[]{:T(128)}, bf16[1,256,128]{2,1,0:T(8,128)(2,1)S(1)}, ...), condition=%wide.region_7.0_spmd.clone, body=%wide.region_6.0_spmd.clone.sunk | while | flops 50790400 | bytes 1968312 | solution.py:91
  70.7 0.2 fusion.52
  70.9 1.7 collective-permute-start.1
  72.8 2.1 collective-permute-done.1
  75.0 0.2 fusion.51
  75.2 0.2 fusion.52
  75.4 1.7 collective-permute-start.1
  77.3 2.1 collective-permute-done.1
  79.5 0.2 fusion.51
  79.7 0.2 fusion.52
  79.9 1.7 collective-permute-start.1
  81.8 2.1 collective-permute-done.1
  84.0 0.2 fusion.51
  84.2 0.2 fusion.52
  84.4 1.7 collective-permute-start.1
  86.3 2.1 collective-permute-done.1
  88.4 0.7 copy.41
  89.1 59.9 %reduce-scatter.5.cloned.1.call-done = bf16[8,4,128]{2,0,1:T(8,128)(2,1)} async-done(((bf16[8,32,128]{2,0,1:T(8,128)(2,1)}), bf16[8,4,128]{2,0,1:T(8,128)(2,1)}) %reduce-scatter.5.cloned.1.call-update) | async-done | bytes 8208 | tf_op jit(solution)/shard_map/reduce_scatter | solution.py:92
  149.0 1.0 convolution_bitcast_fusion.1
  150.0 0.3 fusion.13
  150.4 1.3 copy.45
  151.8 1.4 fusion.12
  153.2 0.3 convolution_convert_fusion.1
  153.5 0.7 reshape.115
  154.2 133.5 %reduce-scatter.7.cloned.1.call-done = f32[64,128]{1,0:T(8,128)} async-done(((f32[2048,128]{1,0:T(8,128)}), f32[64,128]{1,0:T(8,128)}) %reduce-scatter.7.cloned.1.call-update) | async-done | bytes 32784
  (56 shorter events, 2.5 us)
Async XLA Ops:
  7.2 1.2 copy-start
  7.2 10.0 %copy-start.2 = (bf16[8,4,2048]{2,1,0:T(4,128)(2,1)S(1)}, bf16[8,4,2048]{2,1,0:T(4,128)(2,1)}, u32[]{:S(2)}) copy-start(bf16[8,4,2048]{2,1,0:T(4,128)(2,1)} %param.7) | copy-start | bytes 393220
  7.2 141.8 %reduce-scatter.5.cloned.1.call-start = ((), (), s32[]{:S(2)}) async-start(), calls=%async_computation.2 | async-start | bytes 73728 | tf_op jit(solution)/shard_map/reduce_scatter | solution.py:92
  8.4 8.8 %copy-start.1 = (bf16[2048,128]{1,0:T(8,128)(2,1)S(1)}, bf16[2048,128]{1,0:T(8,128)(2,1)}, u32[]{:S(2)}) copy-start(bf16[2048,128]{1,0:T(8,128)(2,1)} %param.9) | copy-start | bytes 1572868
  48.3 21.6 %copy-start.4 = (s32[8,8,2]{1,2,0:T(2,128)S(1)}, s32[8,8,2]{1,2,0:T(2,128)}, u32[]{:S(2)}) copy-start(s32[8,8,2]{1,2,0:T(2,128)} %param.10) | copy-start | bytes 1540
  48.4 21.7 %copy-start.5 = (s32[8,8]{1,0:T(8,128)S(1)}, s32[8,8]{1,0:T(8,128)}, u32[]{:S(2)}) copy-start(s32[8,8]{1,0:T(8,128)} %param.11) | copy-start | bytes 772
  70.4 4.5 %collective-permute-start = (bf16[1,256,128]{2,1,0:T(8,128)(2,1)S(1)}, bf16[1,256,128]{2,1,0:T(8,128)(2,1)S(1)}, u32[]{:S(2)}, u32[]{:S(2)}) collective-permute-start(bf16[1,256,128]{2,1,0:T(8,128)(2,1)S(1)} %copy.56), channel_id=1, source_target_pairs={{0,8},{8,16},{16,24},{24,0},{1,9},{9,17},{17,25},{25,1},{2,10},{10... | collective-permute-start | bytes 196616 | tf_op jit(solution)/shard_map/while/body/eval_jaxpr/ppermute | solution.py:12
  70.9 3.9 %collective-permute-start.1 = (bf16[1,256,128]{2,1,0:T(8,128)(2,1)S(1)}, bf16[1,256,128]{2,1,0:T(8,128)(2,1)S(1)}, u32[]{:S(2)}, u32[]{:S(2)}) collective-permute-start(bf16[1,256,128]{2,1,0:T(8,128)(2,1)S(1)} %fusion.52), channel_id=1, source_target_pairs={{0,8},{8,16},{16,24},{24,0},{1,9},{9,17},{17,25},{25,1},{2,10},{10... | collective-permute-start | bytes 196616 | tf_op jit(solution)/shard_map/while/body/eval_jaxpr/ppermute | solution.py:12
  74.9 4.5 %collective-permute-start = (bf16[1,256,128]{2,1,0:T(8,128)(2,1)S(1)}, bf16[1,256,128]{2,1,0:T(8,128)(2,1)S(1)}, u32[]{:S(2)}, u32[]{:S(2)}) collective-permute-start(bf16[1,256,128]{2,1,0:T(8,128)(2,1)S(1)} %copy.56), channel_id=1, source_target_pairs={{0,8},{8,16},{16,24},{24,0},{1,9},{9,17},{17,25},{25,1},{2,10},{10... | collective-permute-start | bytes 196616 | tf_op jit(solution)/shard_map/while/body/eval_jaxpr/ppermute | solution.py:12
  75.4 3.9 %collective-permute-start.1 = (bf16[1,256,128]{2,1,0:T(8,128)(2,1)S(1)}, bf16[1,256,128]{2,1,0:T(8,128)(2,1)S(1)}, u32[]{:S(2)}, u32[]{:S(2)}) collective-permute-start(bf16[1,256,128]{2,1,0:T(8,128)(2,1)S(1)} %fusion.52), channel_id=1, source_target_pairs={{0,8},{8,16},{16,24},{24,0},{1,9},{9,17},{17,25},{25,1},{2,10},{10... | collective-permute-start | bytes 196616 | tf_op jit(solution)/shard_map/while/body/eval_jaxpr/ppermute | solution.py:12
  79.4 4.5 %collective-permute-start = (bf16[1,256,128]{2,1,0:T(8,128)(2,1)S(1)}, bf16[1,256,128]{2,1,0:T(8,128)(2,1)S(1)}, u32[]{:S(2)}, u32[]{:S(2)}) collective-permute-start(bf16[1,256,128]{2,1,0:T(8,128)(2,1)S(1)} %copy.56), channel_id=1, source_target_pairs={{0,8},{8,16},{16,24},{24,0},{1,9},{9,17},{17,25},{25,1},{2,10},{10... | collective-permute-start | bytes 196616 | tf_op jit(solution)/shard_map/while/body/eval_jaxpr/ppermute | solution.py:12
  79.9 3.9 %collective-permute-start.1 = (bf16[1,256,128]{2,1,0:T(8,128)(2,1)S(1)}, bf16[1,256,128]{2,1,0:T(8,128)(2,1)S(1)}, u32[]{:S(2)}, u32[]{:S(2)}) collective-permute-start(bf16[1,256,128]{2,1,0:T(8,128)(2,1)S(1)} %fusion.52), channel_id=1, source_target_pairs={{0,8},{8,16},{16,24},{24,0},{1,9},{9,17},{17,25},{25,1},{2,10},{10... | collective-permute-start | bytes 196616 | tf_op jit(solution)/shard_map/while/body/eval_jaxpr/ppermute | solution.py:12
  83.9 4.5 %collective-permute-start = (bf16[1,256,128]{2,1,0:T(8,128)(2,1)S(1)}, bf16[1,256,128]{2,1,0:T(8,128)(2,1)S(1)}, u32[]{:S(2)}, u32[]{:S(2)}) collective-permute-start(bf16[1,256,128]{2,1,0:T(8,128)(2,1)S(1)} %copy.56), channel_id=1, source_target_pairs={{0,8},{8,16},{16,24},{24,0},{1,9},{9,17},{17,25},{25,1},{2,10},{10... | collective-permute-start | bytes 196616 | tf_op jit(solution)/shard_map/while/body/eval_jaxpr/ppermute | solution.py:12
  84.4 3.9 %collective-permute-start.1 = (bf16[1,256,128]{2,1,0:T(8,128)(2,1)S(1)}, bf16[1,256,128]{2,1,0:T(8,128)(2,1)S(1)}, u32[]{:S(2)}, u32[]{:S(2)}) collective-permute-start(bf16[1,256,128]{2,1,0:T(8,128)(2,1)S(1)} %fusion.52), channel_id=1, source_target_pairs={{0,8},{8,16},{16,24},{24,0},{1,9},{9,17},{17,25},{25,1},{2,10},{10... | collective-permute-start | bytes 196616 | tf_op jit(solution)/shard_map/while/body/eval_jaxpr/ppermute | solution.py:12
  89.1 198.6 %reduce-scatter.7.cloned.1.call-start = ((), (), s32[]{:S(2)}) async-start(), calls=%async_computation.3 | async-start | bytes 1081344
  151.7 1.4 copy-start.3
Sparse Core Ops, SparseCore 0:
  89.2 59.7 reduce-scatter.4
  151.9 135.8 reduce-scatter.6
where the time goes:
time: 295 us
  waiting for transfers between devices  202 us (68%)
  blocking collectives  58.6 us (20%)
  between operations  14.2 us (5%)
  matrix products  7.66 us (3%)
  starting transfers between devices  6.98 us (2%)
  local copies, waits for them, and re-layouts  4.37 us (1%)
    unnamed x3, waiting for transfers between devices  134 us
    reduce_scatter x1, waiting for transfers between devices, shards(): lax.psum_scatter(token_acc.reshape(query_count, query_tokens, embed_width...  59.9 us
    all_gather x1, blocking collectives, shards(): lax.all_gather(own_embed, 'pa', axis=1, tiled=True).reshape(-1, embed_width)  30.9 us
    all_gather x1, blocking collectives, shards(): score_table = lax.all_gather(query_score, 'pa', axis=1, tiled=True)  20.5 us
    ppermute x8, waiting for transfers between devices, from_behind(): return lax.ppermute(value, axis, pairs)  8.25 us
    all_gather x1, blocking collectives, shards(): lax.all_gather(page_embed, 'pb', axis=1, tiled=True)[0]  7.25 us
    ppermute x8, starting transfers between devices, from_behind(): return lax.ppermute(value, axis, pairs)  6.9 us
  transfers between devices with their start and end apart: 10, of which 6 were waited for; matrix products, arithmetic and copies ran while one was open for 2% of the time, Pallas kernels for 0%

commit v1 on v0

--- a/solution.py
+++ b/solution.py
@@ -26,7 +26,7 @@
         query_hidden.reshape(-1, hidden_width), projection, preferred_element_type=jnp.float32
     ).astype(jnp.bfloat16)
     own_embed = own_embed.reshape(query_count, token_local, embed_width)
-    tok_rows = lax.all_gather(own_embed, "pa", axis=1, tiled=True).reshape(-1, embed_width)
+    tok_rows = jnp.concatenate(lax.all_gather(own_embed, "pa"), axis=1).reshape(-1, embed_width)
     row_count = tok_rows.shape[0]
     query_tokens = row_count // query_count
     page_embed = jnp.dot(

time: 295 us -> 295 us (level)
  no operation moved by 1% of the time
where the time goes in v1:
time: 295 us; the launch traced here: 294 us
  waiting for transfers between devices  202 us (68%)
  blocking collectives  58.6 us (20%)
  between operations  14.2 us (5%)
  matrix products  7.65 us (3%)
  starting transfers between devices  6.98 us (2%)
  local copies, waits for them, and re-layouts  4.39 us (1%)
    unnamed x3, waiting for transfers between devices  133 us
    reduce_scatter x1, waiting for transfers between devices, shards(): lax.psum_scatter(token_acc.reshape(query_count, query_tokens, embed_width...  59.9 us
    all_gather x1, blocking collectives, shards(): lax.all_gather(own_embed, 'pa')  30.9 us
    all_gather x1, blocking collectives, shards(): score_table = lax.all_gather(query_score, 'pa', axis=1, tiled=True)  20.5 us
    ppermute x8, waiting for transfers between devices, from_behind(): return lax.ppermute(value, axis, pairs)  8.26 us
    all_gather x1, blocking collectives, shards(): lax.all_gather(page_embed, 'pb', axis=1, tiled=True)[0]  7.25 us
    ppermute x8, starting transfers between devices, from_behind(): return lax.ppermute(value, axis, pairs)  6.9 us
  transfers between devices with their start and end apart: 10, of which 6 were waited for; matrix products, arithmetic and copies ran while one was open for 2% of the time, Pallas kernels for 0%

profile of v1, /device:TPU:0, one launch (start us, length us, event | category | flops | bytes accessed | tf_op | source)
XLA Modules:
  0.0 294.4 jit_solution(5023919623815478895)
XLA Ops:
  7.2 1.2 copy-done
  8.4 1.5 convolution_convert_fusion.2
  9.9 7.3 %all-gather = bf16[1024,128]{1,0:T(8,128)(2,1)S(1)} all-gather(bf16[256,128]{1,0:T(8,128)(2,1)S(1)} %convolution_convert_fusion.2), channel_id=2, replica_groups=mesh['pb'=4,'pa'=8] {'pb'}, dimensions={0}, use_global_device_ids=true | all-gather | bytes 327680 | tf_op jit(solution)/shard_map/all_gather | solution.py:41
  17.5 30.9 %all_gather.9 = bf16[8,8,4,128]{3,1,2,0:T(8,128)(2,1)S(1)} all-gather(bf16[1,8,4,128]{3,1,2,0:T(8,128)(2,1)S(1)} %copy.38), channel_id=1, replica_groups=mesh['pb'=4,'pa'=8] {'pa'}, dimensions={0}, use_global_device_ids=true | all-gather | bytes 73728 | tf_op jit(solution)/shard_map/all_gather | solution.py:29
  48.4 0.4 fusion.24
  48.8 0.3 exponential_reduce_fusion
  49.4 20.5 %all-gather.1 = f32[8,1,8]{2,1,0:T(1,128)S(1)} all-gather(f32[1,1,8]{2,1,0:T(1,128)S(1)} %bitcast.85), channel_id=1, replica_groups=mesh['pb'=4,'pa'=8] {'pa'}, dimensions={0}, use_global_device_ids=true | all-gather | bytes 288 | tf_op jit(solution)/shard_map/all_gather | solution.py:56
  70.4 18.0 %while.15 = (s32[]{:T(128)}, bf16[1,256,128]{2,1,0:T(8,128)(2,1)S(1)}, f32[1,256,128]{2,1,0:T(8,128)S(1)}, f32[256,128]{1,0:T(8,128)S(1)}, bf16[256,128]{1,0:T(8...) while((s32[]{:T(128)}, bf16[1,256,128]{2,1,0:T(8,128)(2,1)S(1)}, ...), condition=%wide.region_7.0_spmd.clone, body=%wide.region_6.0_spmd.clone.sunk | while | flops 50790400 | bytes 1968312 | solution.py:91
  70.5 0.2 fusion.51
  70.7 0.2 fusion.52
  70.9 1.7 collective-permute-start.1
  72.8 2.1 collective-permute-done.1
  75.2 0.2 fusion.52
  75.4 1.7 collective-permute-start.1
  77.3 2.1 collective-permute-done.1
  79.5 0.2 fusion.51
  79.7 0.2 fusion.52
  79.9 1.7 collective-permute-start.1
  81.8 2.1 collective-permute-done.1
  84.0 0.2 fusion.51
  84.2 0.2 fusion.52
  84.4 1.7 collective-permute-start.1
  86.3 2.1 collective-permute-done.1
  88.4 0.7 copy.43
  89.1 59.9 %reduce-scatter.5.cloned.1.call-done = bf16[8,4,128]{2,0,1:T(8,128)(2,1)} async-done(((bf16[8,32,128]{2,0,1:T(8,128)(2,1)}), bf16[8,4,128]{2,0,1:T(8,128)(2,1)}) %reduce-scatter.5.cloned.1.call-update) | async-done | bytes 8208 | tf_op jit(solution)/shard_map/reduce_scatter | solution.py:92
  149.0 1.0 convolution_bitcast_fusion.1
  150.0 0.3 fusion.13
  150.4 1.3 copy.47
  151.7 1.4 fusion.12
  153.2 0.3 convolution_convert_fusion.1
  153.4 0.7 reshape.111
  154.2 133.4 %reduce-scatter.7.cloned.1.call-done = f32[64,128]{1,0:T(8,128)} async-done(((f32[2048,128]{1,0:T(8,128)}), f32[64,128]{1,0:T(8,128)}) %reduce-scatter.7.cloned.1.call-update) | async-done | bytes 32784
  (56 shorter events, 2.5 us)
Async XLA Ops:
  7.2 1.2 copy-start
  7.2 10.0 %copy-start.2 = (bf16[8,4,2048]{2,1,0:T(4,128)(2,1)S(1)}, bf16[8,4,2048]{2,1,0:T(4,128)(2,1)}, u32[]{:S(2)}) copy-start(bf16[8,4,2048]{2,1,0:T(4,128)(2,1)} %param.7) | copy-start | bytes 393220
  7.2 141.8 %reduce-scatter.5.cloned.1.call-start = ((), (), s32[]{:S(2)}) async-start(), calls=%async_computation.2 | async-start | bytes 73728 | tf_op jit(solution)/shard_map/reduce_scatter | solution.py:92
  8.4 8.8 %copy-start.1 = (bf16[2048,128]{1,0:T(8,128)(2,1)S(1)}, bf16[2048,128]{1,0:T(8,128)(2,1)}, u32[]{:S(2)}) copy-start(bf16[2048,128]{1,0:T(8,128)(2,1)} %param.9) | copy-start | bytes 1572868
  48.4 21.6 %copy-start.4 = (s32[8,8,2]{1,2,0:T(2,128)S(1)}, s32[8,8,2]{1,2,0:T(2,128)}, u32[]{:S(2)}) copy-start(s32[8,8,2]{1,2,0:T(2,128)} %param.10) | copy-start | bytes 1540
  48.4 21.7 %copy-start.5 = (s32[8,8]{1,0:T(8,128)S(1)}, s32[8,8]{1,0:T(8,128)}, u32[]{:S(2)}) copy-start(s32[8,8]{1,0:T(8,128)} %param.11) | copy-start | bytes 772
  70.4 4.5 %collective-permute-start = (bf16[1,256,128]{2,1,0:T(8,128)(2,1)S(1)}, bf16[1,256,128]{2,1,0:T(8,128)(2,1)S(1)}, u32[]{:S(2)}, u32[]{:S(2)}) collective-permute-start(bf16[1,256,128]{2,1,0:T(8,128)(2,1)S(1)} %copy.58), channel_id=1, source_target_pairs={{0,8},{8,16},{16,24},{24,0},{1,9},{9,17},{17,25},{25,1},{2,10},{10... | collective-permute-start | bytes 196616 | tf_op jit(solution)/shard_map/while/body/eval_jaxpr/ppermute | solution.py:12
  70.9 3.9 %collective-permute-start.1 = (bf16[1,256,128]{2,1,0:T(8,128)(2,1)S(1)}, bf16[1,256,128]{2,1,0:T(8,128)(2,1)S(1)}, u32[]{:S(2)}, u32[]{:S(2)}) collective-permute-start(bf16[1,256,128]{2,1,0:T(8,128)(2,1)S(1)} %fusion.52), channel_id=1, source_target_pairs={{0,8},{8,16},{16,24},{24,0},{1,9},{9,17},{17,25},{25,1},{2,10},{10... | collective-permute-start | bytes 196616 | tf_op jit(solution)/shard_map/while/body/eval_jaxpr/ppermute | solution.py:12
  74.9 4.5 %collective-permute-start = (bf16[1,256,128]{2,1,0:T(8,128)(2,1)S(1)}, bf16[1,256,128]{2,1,0:T(8,128)(2,1)S(1)}, u32[]{:S(2)}, u32[]{:S(2)}) collective-permute-start(bf16[1,256,128]{2,1,0:T(8,128)(2,1)S(1)} %copy.58), channel_id=1, source_target_pairs={{0,8},{8,16},{16,24},{24,0},{1,9},{9,17},{17,25},{25,1},{2,10},{10... | collective-permute-start | bytes 196616 | tf_op jit(solution)/shard_map/while/body/eval_jaxpr/ppermute | solution.py:12
  75.4 3.9 %collective-permute-start.1 = (bf16[1,256,128]{2,1,0:T(8,128)(2,1)S(1)}, bf16[1,256,128]{2,1,0:T(8,128)(2,1)S(1)}, u32[]{:S(2)}, u32[]{:S(2)}) collective-permute-start(bf16[1,256,128]{2,1,0:T(8,128)(2,1)S(1)} %fusion.52), channel_id=1, source_target_pairs={{0,8},{8,16},{16,24},{24,0},{1,9},{9,17},{17,25},{25,1},{2,10},{10... | collective-permute-start | bytes 196616 | tf_op jit(solution)/shard_map/while/body/eval_jaxpr/ppermute | solution.py:12
  79.4 4.5 %collective-permute-start = (bf16[1,256,128]{2,1,0:T(8,128)(2,1)S(1)}, bf16[1,256,128]{2,1,0:T(8,128)(2,1)S(1)}, u32[]{:S(2)}, u32[]{:S(2)}) collective-permute-start(bf16[1,256,128]{2,1,0:T(8,128)(2,1)S(1)} %copy.58), channel_id=1, source_target_pairs={{0,8},{8,16},{16,24},{24,0},{1,9},{9,17},{17,25},{25,1},{2,10},{10... | collective-permute-start | bytes 196616 | tf_op jit(solution)/shard_map/while/body/eval_jaxpr/ppermute | solution.py:12
  79.9 3.9 %collective-permute-start.1 = (bf16[1,256,128]{2,1,0:T(8,128)(2,1)S(1)}, bf16[1,256,128]{2,1,0:T(8,128)(2,1)S(1)}, u32[]{:S(2)}, u32[]{:S(2)}) collective-permute-start(bf16[1,256,128]{2,1,0:T(8,128)(2,1)S(1)} %fusion.52), channel_id=1, source_target_pairs={{0,8},{8,16},{16,24},{24,0},{1,9},{9,17},{17,25},{25,1},{2,10},{10... | collective-permute-start | bytes 196616 | tf_op jit(solution)/shard_map/while/body/eval_jaxpr/ppermute | solution.py:12
  83.9 4.5 %collective-permute-start = (bf16[1,256,128]{2,1,0:T(8,128)(2,1)S(1)}, bf16[1,256,128]{2,1,0:T(8,128)(2,1)S(1)}, u32[]{:S(2)}, u32[]{:S(2)}) collective-permute-start(bf16[1,256,128]{2,1,0:T(8,128)(2,1)S(1)} %copy.58), channel_id=1, source_target_pairs={{0,8},{8,16},{16,24},{24,0},{1,9},{9,17},{17,25},{25,1},{2,10},{10... | collective-permute-start | bytes 196616 | tf_op jit(solution)/shard_map/while/body/eval_jaxpr/ppermute | solution.py:12
  84.4 3.9 %collective-permute-start.1 = (bf16[1,256,128]{2,1,0:T(8,128)(2,1)S(1)}, bf16[1,256,128]{2,1,0:T(8,128)(2,1)S(1)}, u32[]{:S(2)}, u32[]{:S(2)}) collective-permute-start(bf16[1,256,128]{2,1,0:T(8,128)(2,1)S(1)} %fusion.52), channel_id=1, source_target_pairs={{0,8},{8,16},{16,24},{24,0},{1,9},{9,17},{17,25},{25,1},{2,10},{10... | collective-permute-start | bytes 196616 | tf_op jit(solution)/shard_map/while/body/eval_jaxpr/ppermute | solution.py:12
  89.1 198.5 %reduce-scatter.7.cloned.1.call-start = ((), (), s32[]{:S(2)}) async-start(), calls=%async_computation.3 | async-start | bytes 1081344
  151.7 1.4 copy-start.3
Sparse Core Ops, SparseCore 0:
  89.2 59.7 reduce-scatter.4
  151.9 135.6 reduce-scatter.6
